TPU v7x, 256 devices: a whole 4x4x8 slice. The times are simulated.
256 devices in a mesh: row: 16 (over y_hi, x, core), col: 16 (over z, y_lo).
Axes of the slice: x: 4, y: 4 (y_hi: 2, y_lo: 2; y = y_hi * 2 + y_lo), z: 8, core: 2. Of those that a mesh axis runs over, the one named last changes fastest.
Arguments:
- features: bfloat16 [32768, 512], P(('row', 'col')), may hold values from -6 to 6
- coefs: bfloat16 [32768], P(('row', 'col')), may hold values from -150 to 150
Outputs:
- grads: bfloat16 [32768, 512], P(('row', 'col'))
- recolored: bfloat16 [32768, 512], P(('row', 'col'))
All inputs are finite; a program needn't handle non-finite values.
Results may differ from a plain program's by a relative error of at most 0.0025.
The roundings to bfloat16 on the way count: a program that leaves them out, or rounds other values in their place, can miss the bound.
Values may be sent and summed in bfloat16 or wider, within the bound.
No kernel may reach another device: no remote copies, remote signals or barrier semaphores. Data moves between devices by JAX's collectives and lax.ppermute only.
A program may use at most 64 MiB of HBM per device.

v0:
```python
import jax
import jax.numpy as jnp
from jax import lax
from jax.sharding import PartitionSpec as P


def from_everyone(shard, axis):
    copies = jnp.broadcast_to(shard, (lax.axis_size(axis), *shard.shape))
    return lax.all_to_all(copies, axis, split_axis=0, concat_axis=0, tiled=True)


def laid_out(blocks, dim):
    blocks = jnp.moveaxis(blocks, 0, dim)
    shape = blocks.shape
    return blocks.reshape(*shape[:dim], shape[dim] * shape[dim + 1], *shape[dim + 2 :])


def gather_directly(shard, axis, dim):
    blocks = from_everyone(shard, axis)
    return laid_out(blocks, dim)


def in_blocks(shard, dim, count):
    before, after = (shard.shape[:dim], shard.shape[dim + 1 :])
    return jnp.moveaxis(shard.reshape(*before, count, -1, *after), dim, 0)


def sent_and_summed(shard, axis, dim):
    count = lax.axis_size(axis)
    blocks = lax.all_to_all(in_blocks(shard, dim, count), axis, 0, 0, tiled=True)
    return jnp.sum(blocks, axis=0)


def in_one_piece(arrays, axis, dim, along):
    columns = [a.reshape(*a.shape[:along], -1) for a in arrays]
    both = jnp.concatenate(columns, axis=along)
    result, at, finished = (sent_and_summed(both, axis, dim), 0, [])
    for a, column in zip(arrays, columns):
        section = result[..., at : at + column.shape[along]]
        finished.append(section.reshape(*section.shape[:along], *a.shape[along:]))
        at += column.shape[along]
    return tuple(finished)


def tile_terms(row_points, row_norms, col_points, col_coefs):
    width = row_points.shape[1]
    gamma = 2.0 / width
    col_full = col_points.astype(jnp.float32)
    col_norms = jnp.sum(col_full * col_full, axis=1)
    weighted = (col_coefs.astype(jnp.float32)[:, None] * col_full).astype(jnp.bfloat16)
    row_count = row_points.shape[0]
    strip_len = min(512, row_count)
    strip_count = row_count // strip_len

    def one_strip(packed):
        strip_points, strip_norms = packed
        products = lax.dot_general(
            strip_points, col_points, (((1,), (1,)), ((), ())), preferred_element_type=jnp.float32
        )
        kernel = jnp.exp(
            -(strip_norms[:, None] + col_norms[None, :] - 2.0 * products) * gamma
        ).astype(jnp.bfloat16)
        totals = jnp.dot(kernel, col_coefs, preferred_element_type=jnp.float32)
        moments = jnp.dot(kernel, weighted, preferred_element_type=jnp.float32)
        return (totals, moments)

    totals, moments = lax.map(
        one_strip,
        (
            row_points.reshape(strip_count, strip_len, width),
            row_norms.reshape(strip_count, strip_len),
        ),
    )
    return (totals.reshape(row_count), moments.reshape(row_count, width))


def local(features, coefs):
    width = features.shape[1]
    gamma = 2.0 / width
    row_points = gather_directly(features, "col", 0)
    row_full = row_points.astype(jnp.float32)
    row_norms = jnp.sum(row_full * row_full, axis=1)
    col_points, col_coefs = (
        lax.all_gather(features, "row", axis=0, tiled=True),
        lax.all_gather(coefs, "row", axis=0, tiled=True),
    )
    totals, moments = tile_terms(row_points, row_norms, col_points, col_coefs)
    own_totals, own_moments = in_one_piece((totals, moments), "col", 0, 1)
    own_full = features.astype(jnp.float32)
    grads = (2.0 * gamma * (own_moments - own_totals[:, None] * own_full)).astype(jnp.bfloat16)
    gram = jnp.einsum("pa,pb->ab", grads, grads, preferred_element_type=jnp.float32)
    point_count = features.shape[0] * lax.axis_size("row") * lax.axis_size("col")
    whole_gram = lax.psum(gram, ("row", "col"))
    agop = (whole_gram / point_count).astype(jnp.bfloat16)
    recolored = jnp.dot(features, agop, preferred_element_type=jnp.float32)
    return (grads, recolored.astype(jnp.bfloat16))


def solution(mesh):
    return jax.shard_map(
        local,
        mesh=mesh,
        in_specs=(P(("row", "col"), None), P(("row", "col"))),
        out_specs=(P(("row", "col"), None), P(("row", "col"), None)),
        check_vma=False,
    )
```

profile of v0, /device:TPU:2, one launch (start us, length us, event | category | flops | bytes accessed | tf_op | source)
XLA Modules:
  0.0 500.3 jit_solution(5801225828391039374)
XLA Ops:
  7.2 0.0 copy-start.2
  7.2 2.4 broadcast_in_dim.22
  9.6 9.6 %all-to-all-start = ((bf16[16,128,512]{2,1,0:T(8,128)(2,1)}), bf16[16,128,512]{2,1,0:T(8,128)(2,1)S(1)}, u32[]{:S(2)}, u32[]{:S(2)}) async-start(bf16[16,128,512]{2,1,0:T(8,128)(2,1)} %broadcast_in_dim.22), calls=%async_computation | async-start | bytes 4194304 | tf_op jit(solution)/shard_map/all_to_all | solution.py:9
  19.2 0.0 all-gather.3.cloned.1.call-start
  19.2 0.7 all-gather.3.cloned.1.call-update
  19.9 0.0 copy-done.2
  19.9 19.8 %all-gather = bf16[16,1,128]{2,1,0:T(2,128)(2,1)S(1)} all-gather(bf16[1,1,128]{2,1,0:T(2,128)(2,1)S(1)} %bitcast.46), channel_id=1, replica_groups=mesh['row'=16,'col'=16] {'row'}, dimensions={0}, use_global_device_ids=true | all-gather | bytes 4352 | tf_op jit(solution)/shard_map/all_gather | solution.py:85
  39.7 29.9 %all-to-all-done = bf16[16,128,512]{2,1,0:T(8,128)(2,1)S(1)} async-done(((bf16[16,128,512]{2,1,0:T(8,128)(2,1)}), bf16[16,128,512]{2,1,0:T(8,128)(2,1)S(1)}, u32[]{:S(2)}, u32[]{:S(2)}) %all-to-all-start) | async-done | bytes 2097184 | tf_op jit(solution)/shard_map/all_to_all | solution.py:9
  69.7 0.5 multiply_reduce_fusion
  70.2 14.8 %all-gather.3.cloned.1.call-done = bf16[2048,512]{1,0:T(8,128)(2,1)} async-done(((bf16[128,512]{1,0:T(8,128)(2,1)}), bf16[2048,512]{1,0:T(8,128)(2,1)}) %all-gather.3.cloned.1.call-update) | async-done | bytes 2097168 | tf_op jit(solution)/shard_map/all_gather | solution.py:84
  85.0 3.5 fusion.5
  88.5 24.6 %while.12 = (s32[]{:T(128)}, f32[4,512]{1,0:T(4,128)S(1)}, f32[4,512,512]{2,1,0:T(8,128)}, f32[4,512]{1,0:T(4,128)S(1)}, f32[2048]{0:T(1024)S(1)}, /*index=5*/bf...) while((s32[]{:T(128)}, f32[4,512]{1,0:T(4,128)S(1)}, ...), condition=%wide.region_3.4_spmd, body=%wide.region_2.3_spmd.sunk | while | flops 2155872256 | bytes 20480660 | solution.py:67
  88.5 0.0 copy-start.1
  88.5 3.1 exponential_convert_fusion.2
  91.7 0.0 copy-done.1
  91.7 2.3 fusion.36
  94.0 0.6 fusion.35
  94.7 0.0 copy-start.1
  94.7 3.1 exponential_convert_fusion.2
  97.8 0.0 copy-done.1
  97.8 2.3 fusion.36
  100.1 0.6 fusion.35
  100.8 0.0 copy-start.1
  100.8 3.1 exponential_convert_fusion.2
  104.0 0.0 copy-done.1
  104.0 2.3 fusion.36
  106.3 0.6 fusion.35
  107.0 0.0 copy-start.1
  107.0 3.1 exponential_convert_fusion.2
  110.1 0.0 copy-done.1
  110.1 2.3 fusion.36
  112.5 0.6 fusion.35
  113.2 0.9 concatenate.11
  114.0 5.9 %pad_maximum_fusion = f32[16,128,513]{2,1,0:T(8,128)} fusion(f32[16,128,512]{2,1,0:T(8,128)} %bitcast.43, f32[16,128,1]{2,1,0:T(8,128)S(1)} %concatenate.11), kind=kLoop, calls=%fused_computation.9 | loop fusion | flops 1050624 | bytes 8404992 | tf_op jit(solution)/shard_map/concatenate | solution.py:36
  120.0 5.7 %copy.15 = f32[16,128,513]{1,2,0:T(8,128)} copy(f32[16,128,513]{2,1,0:T(8,128)} %pad_maximum_fusion) | data formatting | bytes 8404992 | tf_op jit(solution)/shard_map/concatenate | solution.py:36
  125.7 0.0 copy-start
  125.7 4.7 all-to-all-start.1
  130.3 0.0 all-reduce.2.cloned.1.call-start
  130.4 0.0 copy-done
  130.4 0.1 copy.16
  130.5 100.1 %all-to-all-done.1 = f32[16,128,513]{1,2,0:T(8,128)} async-done(((f32[16,128,513]{1,2,0:T(8,128)}), f32[16,128,513]{1,2,0:T(8,128)}, u32[]{:S(2)}, u32[]{:S(2)}) %all-to-all-start.1) | async-done | bytes 4202528 | tf_op jit(solution)/shard_map/all_to_all | solution.py:30
  230.6 2.4 reduce_sum.29
  233.1 0.1 fusion.9
  233.1 1.3 fusion.12
  234.5 0.0 all-reduce.2.cloned.1.call-update
  234.5 0.8 copy.17
  235.3 255.8 %all-reduce.2.cloned.1.call-done = f32[512,512]{1,0:T(8,128)} async-done(((f32[512,512]{1,0:T(8,128)}), f32[512,512]{1,0:T(8,128)}) %all-reduce.2.cloned.1.call-update) | async-done | bytes 1048592 | tf_op jit(solution)/shard_map/psum | solution.py:93
  491.1 1.6 fusion.6
  492.7 0.8 copy.18
  (18 shorter events, 0.3 us)
Async XLA Ops:
  7.2 12.8 %copy-start.2 = (bf16[128]{0:T(256)(128)(2,1)S(1)}, bf16[128]{0:T(256)(128)(2,1)}, u32[]{:S(2)}) copy-start(bf16[128]{0:T(256)(128)(2,1)} %param.5) | copy-start | bytes 772
  9.6 60.1 %all-to-all-start = ((bf16[16,128,512]{2,1,0:T(8,128)(2,1)}), bf16[16,128,512]{2,1,0:T(8,128)(2,1)S(1)}, u32[]{:S(2)}, u32[]{:S(2)}) async-start(bf16[16,128,512]{2,1,0:T(8,128)(2,1)} %broadcast_in_dim.22), calls=%async_computation | async-start | bytes 4194304 | tf_op jit(solution)/shard_map/all_to_all | solution.py:9
  19.2 65.8 %all-gather.3.cloned.1.call-start = ((), (), s32[]{:S(2)}) async-start(), calls=%async_computation.2 | async-start | bytes 2228224 | tf_op jit(solution)/shard_map/all_gather | solution.py:84
  88.5 3.1 copy-start.1
  94.7 3.2 copy-start.1
  100.8 3.2 copy-start.1
  107.0 3.2 copy-start.1
  125.7 4.7 copy-start
  125.7 104.9 %all-to-all-start.1 = ((f32[16,128,513]{1,2,0:T(8,128)}), f32[16,128,513]{1,2,0:T(8,128)}, u32[]{:S(2)}, u32[]{:S(2)}) async-start(f32[16,128,513]{1,2,0:T(8,128)} %copy.15), calls=%async_computation.1 | async-start | bytes 8519680 | tf_op jit(solution)/shard_map/all_to_all | solution.py:30
  130.3 360.7 %all-reduce.2.cloned.1.call-start = ((), (), s32[]{:S(2)}) async-start(), calls=%async_computation.3 | async-start | bytes 2097152 | tf_op jit(solution)/shard_map/psum | solution.py:93
Sparse Core Ops, SparseCore 0:
  22.7 62.2 all-gather.2
  234.6 256.4 all-reduce.1
where the time goes:
time: 501 us; the launch traced here: 500 us
  waiting for transfers between devices  401 us (80%)
  matrix products  27.1 us (5%)
  blocking collectives  19.8 us (4%)
  starting transfers between devices  14.3 us (3%)
  between operations  14.1 us (3%)
  other arithmetic  12.5 us (2%)
  local copies, waits for them, and re-layouts  10.9 us (2%)
    psum x1, waiting for transfers between devices, local(): whole_gram = lax.psum(gram, ('row', 'col'))  256 us
    all_to_all x1, waiting for transfers between devices, sent_and_summed(): lax.all_to_all(in_blocks(shard, dim, count), axis, 0, 0, tiled=True)  100 us
    all_to_all x1, waiting for transfers between devices, from_everyone(): return lax.all_to_all(copies, axis, split_axis=0, concat_axis=0, tiled=True)  29.9 us
    all_gather x1, blocking collectives, local(): lax.all_gather(coefs, 'row', axis=0, tiled=True)  19.8 us
    all_gather x1, waiting for transfers between devices, local(): lax.all_gather(features, 'row', axis=0, tiled=True)  14.8 us
    dot_general x4, matrix products, one_strip(): lax.dot_general(strip_points, col_points, (((1,), (1,)), ((), ())), prefe...  12.5 us
  transfers between devices with their start and end apart: 4, of which 4 were waited for; matrix products, arithmetic and copies ran while one was open for 0% of the time, Pallas kernels for 0%

commit v1 on v0

--- a/solution.py
+++ b/solution.py
@@ -90,7 +90,7 @@
     grads = (2.0 * gamma * (own_moments - own_totals[:, None] * own_full)).astype(jnp.bfloat16)
     gram = jnp.einsum("pa,pb->ab", grads, grads, preferred_element_type=jnp.float32)
     point_count = features.shape[0] * lax.axis_size("row") * lax.axis_size("col")
-    whole_gram = lax.psum(gram, ("row", "col"))
+    whole_gram = lax.psum(lax.psum(gram, "col"), "row")
     agop = (whole_gram / point_count).astype(jnp.bfloat16)
     recolored = jnp.dot(features, agop, preferred_element_type=jnp.float32)
     return (grads, recolored.astype(jnp.bfloat16))

time: 501 us -> 531 us (1.060); the launches traced: 500 us -> 525 us
  waiting for transfers between devices: 401 us -> 426 us
    psum x1 -> x2, waiting for transfers between devices: 256 us -> 281 us  [local(): whole_gram = lax.psum(lax.psum(gram, 'col'), 'row')]
  transfers between devices with their start and end apart: 4 -> 5, of which waited for: 4 -> 5; matrix products, arithmetic and copies ran while one was open for 0% -> 0% of each run, Pallas kernels for 0% -> 0%
where the time goes in v1:
time: 531 us; the launch traced here: 525 us
  waiting for transfers between devices  426 us (80%)
  matrix products  27.1 us (5%)
  blocking collectives  19.8 us (4%)
  starting transfers between devices  14.4 us (3%)
  between operations  13.9 us (3%)
  other arithmetic  12.5 us (2%)
  local copies, waits for them, and re-layouts  10.9 us (2%)
    psum x2, waiting for transfers between devices, local(): whole_gram = lax.psum(lax.psum(gram, 'col'), 'row')  281 us
    all_to_all x1, waiting for transfers between devices, sent_and_summed(): lax.all_to_all(in_blocks(shard, dim, count), axis, 0, 0, tiled=True)  100 us
    all_to_all x1, waiting for transfers between devices, from_everyone(): return lax.all_to_all(copies, axis, split_axis=0, concat_axis=0, tiled=True)  29.9 us
    all_gather x1, blocking collectives, local(): lax.all_gather(coefs, 'row', axis=0, tiled=True)  19.8 us
    all_gather x1, waiting for transfers between devices, local(): lax.all_gather(features, 'row', axis=0, tiled=True)  14.8 us
    dot_general x4, matrix products, one_strip(): lax.dot_general(strip_points, col_points, (((1,), (1,)), ((), ())), prefe...  12.5 us
  transfers between devices with their start and end apart: 5, of which 5 were waited for; matrix products, arithmetic and copies ran while one was open for 0% of the time, Pallas kernels for 0%

profile of v1, /device:TPU:2, one launch (start us, length us, event | category | flops | bytes accessed | tf_op | source)
XLA Modules:
  0.0 524.9 jit_solution(13683975245539323691)
XLA Ops:
  7.2 0.0 copy-start.2
  7.2 2.4 broadcast_in_dim.22
  9.6 9.6 %all-to-all-start = ((bf16[16,128,512]{2,1,0:T(8,128)(2,1)}), bf16[16,128,512]{2,1,0:T(8,128)(2,1)S(1)}, u32[]{:S(2)}, u32[]{:S(2)}) async-start(bf16[16,128,512]{2,1,0:T(8,128)(2,1)} %broadcast_in_dim.22), calls=%async_computation | async-start | bytes 4194304 | tf_op jit(solution)/shard_map/all_to_all | solution.py:9
  19.2 0.0 all-gather.3.cloned.1.call-start
  19.2 0.7 all-gather.3.cloned.1.call-update
  19.9 0.0 copy-done.2
  19.9 19.8 %all-gather = bf16[16,1,128]{2,1,0:T(2,128)(2,1)S(1)} all-gather(bf16[1,1,128]{2,1,0:T(2,128)(2,1)S(1)} %bitcast.46), channel_id=1, replica_groups=mesh['row'=16,'col'=16] {'row'}, dimensions={0}, use_global_device_ids=true | all-gather | bytes 4352 | tf_op jit(solution)/shard_map/all_gather | solution.py:85
  39.7 29.9 %all-to-all-done = bf16[16,128,512]{2,1,0:T(8,128)(2,1)S(1)} async-done(((bf16[16,128,512]{2,1,0:T(8,128)(2,1)}), bf16[16,128,512]{2,1,0:T(8,128)(2,1)S(1)}, u32[]{:S(2)}, u32[]{:S(2)}) %all-to-all-start) | async-done | bytes 2097184 | tf_op jit(solution)/shard_map/all_to_all | solution.py:9
  69.7 0.5 multiply_reduce_fusion
  70.2 14.8 %all-gather.3.cloned.1.call-done = bf16[2048,512]{1,0:T(8,128)(2,1)} async-done(((bf16[128,512]{1,0:T(8,128)(2,1)}), bf16[2048,512]{1,0:T(8,128)(2,1)}) %all-gather.3.cloned.1.call-update) | async-done | bytes 2097168 | tf_op jit(solution)/shard_map/all_gather | solution.py:84
  85.0 3.5 fusion.5
  88.5 24.6 %while.12 = (s32[]{:T(128)}, f32[4,512]{1,0:T(4,128)S(1)}, f32[4,512,512]{2,1,0:T(8,128)}, f32[4,512]{1,0:T(4,128)S(1)}, f32[2048]{0:T(1024)S(1)}, /*index=5*/bf...) while((s32[]{:T(128)}, f32[4,512]{1,0:T(4,128)S(1)}, ...), condition=%wide.region_3.4_spmd, body=%wide.region_2.3_spmd.sunk | while | flops 2155872256 | bytes 20480660 | solution.py:67
  88.5 0.0 copy-start.1
  88.5 3.1 exponential_convert_fusion.2
  91.7 0.0 copy-done.1
  91.7 2.3 fusion.36
  94.0 0.6 fusion.35
  94.7 0.0 copy-start.1
  94.7 3.1 exponential_convert_fusion.2
  97.8 0.0 copy-done.1
  97.8 2.3 fusion.36
  100.1 0.6 fusion.35
  100.8 0.0 copy-start.1
  100.8 3.1 exponential_convert_fusion.2
  104.0 0.0 copy-done.1
  104.0 2.2 fusion.36
  106.3 0.6 fusion.35
  107.0 0.0 copy-start.1
  107.0 3.1 exponential_convert_fusion.2
  110.1 0.0 copy-done.1
  110.1 2.3 fusion.36
  112.5 0.6 fusion.35
  113.2 0.9 concatenate.11
  114.1 5.9 %pad_maximum_fusion = f32[16,128,513]{2,1,0:T(8,128)} fusion(f32[16,128,512]{2,1,0:T(8,128)} %bitcast.43, f32[16,128,1]{2,1,0:T(8,128)S(1)} %concatenate.11), kind=kLoop, calls=%fused_computation.9 | loop fusion | flops 1050624 | bytes 8404992 | tf_op jit(solution)/shard_map/concatenate | solution.py:36
  120.0 5.7 %copy.15 = f32[16,128,513]{1,2,0:T(8,128)} copy(f32[16,128,513]{2,1,0:T(8,128)} %pad_maximum_fusion) | data formatting | bytes 8404992 | tf_op jit(solution)/shard_map/concatenate | solution.py:36
  125.7 0.0 copy-start
  125.7 4.7 all-to-all-start.1
  130.4 0.0 all-reduce.3.cloned.1.call-start
  130.4 0.0 copy-done
  130.4 0.1 copy.16
  130.5 100.1 %all-to-all-done.1 = f32[16,128,513]{1,2,0:T(8,128)} async-done(((f32[16,128,513]{1,2,0:T(8,128)}), f32[16,128,513]{1,2,0:T(8,128)}, u32[]{:S(2)}, u32[]{:S(2)}) %all-to-all-start.1) | async-done | bytes 4202528 | tf_op jit(solution)/shard_map/all_to_all | solution.py:30
  230.6 2.4 reduce_sum.29
  233.0 0.1 fusion.9
  233.1 1.3 fusion.12
  234.4 0.0 all-reduce.3.cloned.1.call-update
  234.5 0.0 all-reduce.5.cloned.1.call-start
  234.5 137.5 %all-reduce.3.cloned.1.call-done = f32[512,512]{1,0:T(8,128)} async-done(((f32[512,512]{1,0:T(8,128)}), f32[512,512]{1,0:T(8,128)}) %all-reduce.3.cloned.1.call-update) | async-done | bytes 1048592 | tf_op jit(solution)/shard_map/psum | solution.py:93
  372.1 0.0 all-reduce.5.cloned.1.call-update
  372.1 0.8 copy.17
  372.8 143.2 %all-reduce.5.cloned.1.call-done = f32[512,512]{1,0:T(8,128)} async-done(((f32[512,512]{1,0:T(8,128)}), f32[512,512]{1,0:T(8,128)}) %all-reduce.5.cloned.1.call-update) | async-done | bytes 1048592 | tf_op jit(solution)/shard_map/psum | solution.py:93
  516.1 1.6 fusion.6
  517.6 0.8 copy.18
  (18 shorter events, 0.3 us)
Async XLA Ops:
  7.2 12.8 %copy-start.2 = (bf16[128]{0:T(256)(128)(2,1)S(1)}, bf16[128]{0:T(256)(128)(2,1)}, u32[]{:S(2)}) copy-start(bf16[128]{0:T(256)(128)(2,1)} %param.5) | copy-start | bytes 772
  9.6 60.1 %all-to-all-start = ((bf16[16,128,512]{2,1,0:T(8,128)(2,1)}), bf16[16,128,512]{2,1,0:T(8,128)(2,1)S(1)}, u32[]{:S(2)}, u32[]{:S(2)}) async-start(bf16[16,128,512]{2,1,0:T(8,128)(2,1)} %broadcast_in_dim.22), calls=%async_computation | async-start | bytes 4194304 | tf_op jit(solution)/shard_map/all_to_all | solution.py:9
  19.2 65.8 %all-gather.3.cloned.1.call-start = ((), (), s32[]{:S(2)}) async-start(), calls=%async_computation.2 | async-start | bytes 2228224 | tf_op jit(solution)/shard_map/all_gather | solution.py:84
  88.5 3.1 copy-start.1
  94.7 3.2 copy-start.1
  100.8 3.2 copy-start.1
  107.0 3.2 copy-start.1
  125.7 4.7 copy-start
  125.7 104.9 %all-to-all-start.1 = ((f32[16,128,513]{1,2,0:T(8,128)}), f32[16,128,513]{1,2,0:T(8,128)}, u32[]{:S(2)}, u32[]{:S(2)}) async-start(f32[16,128,513]{1,2,0:T(8,128)} %copy.15), calls=%async_computation.1 | async-start | bytes 8519680 | tf_op jit(solution)/shard_map/all_to_all | solution.py:30
  130.4 241.7 %all-reduce.3.cloned.1.call-start = ((), (), s32[]{:S(2)}) async-start(), calls=%async_computation.3 | async-start | bytes 2097152 | tf_op jit(solution)/shard_map/psum | solution.py:93
  234.5 281.6 %all-reduce.5.cloned.1.call-start = ((), (), s32[]{:S(2)}) async-start(), calls=%async_computation.4 | async-start | bytes 2097152 | tf_op jit(solution)/shard_map/psum | solution.py:93
Sparse Core Ops, SparseCore 0:
  22.7 62.2 all-gather.2
  234.6 137.4 all-reduce.2
  374.7 141.3 all-reduce.4
